TPU v7x, 32 devices: a whole 2x2x4 slice. The times are simulated.
32 devices in a mesh: rows: 32 (over z, y, x, core).
Axes of the slice: x: 2, y: 2, z: 4, core: 2. Of those that a mesh axis runs over, the one named last changes fastest.
Arguments:
- left_factor: float32 [65536, 1024], P('rows'), may hold values from -6 to 6
- right_factor: float32 [65536, 1024], P('rows'), may hold values from -6 to 6
- tile_counts: int32 [32], P('rows'), may hold values from 1 to 4, as said below
- start_basis: float32 [1024, 256], replicated, may hold values from -6 to 6
Outputs:
- left_proj: float32 [65536, 256], P('rows')
- right_proj: float32 [65536, 256], P('rows')
Inputs may be any that keep to these rules, and one draw needn't show every extreme that they name: `tile_counts`: each device's live slots are its first ones; some device has 4 live slots and some device has 1.
All inputs are finite; a program needn't handle non-finite values.
Results may differ from a plain program's by a relative error of at most 0.0002.
Values sent between devices are 32-bit elements; how exact they have to be, the bound alone decides.
A program may use at most 128 MiB of HBM per device.

v0:
```python
import jax
import jax.numpy as jnp
from jax import lax
from jax.sharding import PartitionSpec as P

RANK = 256
SLOTS = 4
POWER = 2


def product(left_side, right_side):
    return jnp.dot(
        left_side, right_side, precision=lax.Precision.HIGHEST, preferred_element_type=jnp.float32
    )


def transposed_product(left_side, right_side):
    return lax.dot_general(
        left_side,
        right_side,
        (((0,), (0,)), ((), ())),
        precision=lax.Precision.HIGHEST,
        preferred_element_type=jnp.float32,
    )


def right_solve(factor, block):
    return jax.scipy.linalg.solve_triangular(factor, block.T, lower=True).T


def orthonormal(block):
    factor = jnp.linalg.cholesky(transposed_product(block, block))
    return right_solve(factor, block)


def gram_term(left_factor, masked_right):
    return transposed_product(left_factor, masked_right)


def project(factor_rows, mapping, row_mask):
    return product(factor_rows, mapping) * row_mask


def local(left_factor, right_factor, tile_counts, start_basis):
    tile_rows = left_factor.shape[0] // SLOTS
    live_count = tile_counts[0]
    slot_ids = lax.broadcasted_iota(jnp.int32, (SLOTS, 1, 1), 0)
    live_slots = (slot_ids < live_count).astype(jnp.float32)
    row_mask = jnp.broadcast_to(live_slots, (SLOTS, tile_rows, 1)).reshape(-1, 1)
    masked_right = right_factor * row_mask
    current = start_basis
    gram_matrix = lax.psum(gram_term(left_factor, masked_right), "rows")
    for iteration in range(POWER):
        current = orthonormal(transposed_product(gram_matrix, product(gram_matrix, current)))
    image_cols = product(gram_matrix, current)
    square = transposed_product(image_cols, image_cols)
    factor = jnp.linalg.cholesky(square)
    left_map = right_solve(factor, image_cols)
    scaling = jnp.sqrt(jnp.trace(square) / RANK)
    right_map = right_solve(factor, current) * scaling
    left_proj = project(left_factor, left_map, row_mask)
    right_proj = project(right_factor, right_map, row_mask)
    return (left_proj, right_proj)


def solution(mesh):
    return jax.shard_map(
        local,
        mesh=mesh,
        in_specs=(P("rows", None), P("rows", None), P("rows"), P()),
        out_specs=(P("rows", None), P("rows", None)),
        check_vma=False,
    )
```

profile of v0, /device:TPU:0, one launch (start us, length us, event | category | flops | bytes accessed | tf_op | source)
XLA Modules:
  0.0 455.7 jit_solution(5911906269072735339)
XLA Ops:
  8.0 33.5 %fusion.5 = f32[1024,1024]{0,1:T(8,128)} fusion(f32[2048,1024]{1,0:T(8,128)} %param.7, f32[2048,1024]{1,0:T(8,128)} %param.8, f32[2048]{0:T(1024)S(1)} %bitcast.140), kind=kOutput, calls=%fused_computation.13 | convolution fusion | flops 25771900928 | bytes 20979712 | tf_op jit(solution)/shard_map/dot_general | solution.py:18
  41.5 145.1 %all-reduce.3.cloned.1.call-done = f32[1024,1024]{0,1:T(8,128)} async-done(((f32[1024,1024]{0,1:T(8,128)}), f32[1024,1024]{0,1:T(8,128)}) %all-reduce.3.cloned.1.call-update) | async-done | bytes 4194320 | tf_op jit(solution)/shard_map/psum | solution.py:52
  186.7 9.1 %fusion.64 = f32[1024,256]{1,0:T(8,128)S(1)} fusion(f32[1024,1024]{0,1:T(8,128)} %all-reduce.3.cloned.1.call-done, f32[1024,256]{1,0:T(8,128)S(1)} %copy-done), kind=kOutput, calls=%fused_computation.115 | convolution fusion | flops 3221225472 | bytes 6291456 | tf_op jit(solution)/shard_map/dot_general | solution.py:12
  195.8 3.4 fusion.65
  201.2 11.7 %cholesky.172 = f32[128,128]{1,0:T(8,128)S(1)} custom-call(f32[128,128]{1,0:T(8,128)S(1)} %cholesky.270), custom_call_target="Cholesky" | custom-call | tf_op jit(solution)/shard_map/jit(cholesky)/cholesky | solution.py:32
  213.0 9.8 %custom-call.16 = f32[1,128,128]{1,2,0:T(8,128)S(1)} custom-call(f32[1,128,128]{2,1,0:T(8,128)S(1)} %get-tuple-element.79), custom_call_target="InvertDiagBlocksLowerTriangular" | custom-call | tf_op jit(solution)/shard_map/jit(cholesky)/cholesky | solution.py:32
  223.3 11.9 %cholesky.189 = f32[128,128]{1,0:T(8,128)S(1)} custom-call(f32[128,128]{1,0:T(8,128)S(1)} %convolution_subtract_fusion.6), custom_call_target="Cholesky" | custom-call | tf_op jit(solution)/shard_map/jit(cholesky)/cholesky | solution.py:32
  237.2 3.9 while.8
  241.1 19.7 %custom-call.17 = f32[2,128,128]{1,2,0:T(8,128)S(1)} custom-call(f32[2,128,128]{2,1,0:T(8,128)S(1)} %get-tuple-element.30), custom_call_target="InvertDiagBlocksLowerTriangular" | custom-call | tf_op jit(solution)/shard_map/jit(_solve_triangular)/triangular_solve | solution.py:28
  263.1 8.7 %fusion.8 = f32[1024,256]{1,0:T(8,128)S(1)} fusion(f32[1024,1024]{0,1:T(8,128)} %all-reduce.3.cloned.1.call-done, f32[128,1024]{1,0:T(8,128)S(1)} %fusion.38, f32[128,1024]{1,0:T(8,128)S(1)} %fusion.25), kind=kOutput, calls=%fused_computation.21 | convolution fusion | flops 3221487616 | bytes 6291456 | tf_op jit(solution)/shard_map/dot_general | solution.py:12
  271.9 3.4 fusion.67
  277.3 11.7 %cholesky.206 = f32[128,128]{1,0:T(8,128)S(1)} custom-call(f32[128,128]{1,0:T(8,128)S(1)} %cholesky.273), custom_call_target="Cholesky" | custom-call | tf_op jit(solution)/shard_map/jit(cholesky)/cholesky | solution.py:32
  289.1 9.8 %custom-call.18 = f32[1,128,128]{1,2,0:T(8,128)S(1)} custom-call(f32[1,128,128]{2,1,0:T(8,128)S(1)} %get-tuple-element.75), custom_call_target="InvertDiagBlocksLowerTriangular" | custom-call | tf_op jit(solution)/shard_map/jit(cholesky)/cholesky | solution.py:32
  299.4 12.1 %cholesky.223 = f32[128,128]{1,0:T(8,128)S(1)} custom-call(f32[128,128]{1,0:T(8,128)S(1)} %convolution_subtract_fusion.5), custom_call_target="Cholesky" | custom-call | tf_op jit(solution)/shard_map/jit(cholesky)/cholesky | solution.py:32
  314.2 3.9 while.9
  318.1 19.7 %custom-call.19 = f32[2,128,128]{1,2,0:T(8,128)S(1)} custom-call(f32[2,128,128]{2,1,0:T(8,128)S(1)} %get-tuple-element.31), custom_call_target="InvertDiagBlocksLowerTriangular" | custom-call | tf_op jit(solution)/shard_map/jit(_solve_triangular)/triangular_solve | solution.py:28
  340.1 8.6 %fusion.12 = f32[1024,256]{1,0:T(8,128)S(1)} fusion(f32[1024,1024]{0,1:T(8,128)} %all-reduce.3.cloned.1.call-done, f32[128,1024]{1,0:T(8,128)S(1)} %fusion.34, f32[128,1024]{1,0:T(8,128)S(1)} %fusion.23), kind=kOutput, calls=%fused_computation.25 | convolution fusion | flops 3221487616 | bytes 6291456 | tf_op jit(solution)/shard_map/dot_general | solution.py:12
  353.8 11.7 %cholesky.240 = f32[128,128]{1,0:T(8,128)S(1)} custom-call(f32[128,128]{1,0:T(8,128)S(1)} %cholesky.276), custom_call_target="Cholesky" | custom-call | tf_op jit(solution)/shard_map/jit(cholesky)/cholesky | solution.py:57
  365.6 9.8 %custom-call.20 = f32[1,128,128]{1,2,0:T(8,128)S(1)} custom-call(f32[1,128,128]{2,1,0:T(8,128)S(1)} %get-tuple-element.71), custom_call_target="InvertDiagBlocksLowerTriangular" | custom-call | tf_op jit(solution)/shard_map/jit(cholesky)/cholesky | solution.py:57
  377.6 11.7 %cholesky.257 = f32[128,128]{1,0:T(8,128)S(1)} custom-call(f32[128,128]{1,0:T(8,128)S(1)} %convolution_subtract_fusion.4), custom_call_target="Cholesky" | custom-call | tf_op jit(solution)/shard_map/jit(cholesky)/cholesky | solution.py:57
  393.0 3.8 while.10
  397.5 20.5 %custom-call.21 = f32[2,128,128]{1,2,0:T(8,128)S(1)} custom-call(f32[2,128,128]{2,1,0:T(8,128)} %copy-done.6), custom_call_target="InvertDiagBlocksLowerTriangular" | custom-call | tf_op jit(solution)/shard_map/jit(_solve_triangular)/triangular_solve | solution.py:28
  420.8 10.7 %fusion.3 = f32[2048,256]{0,1:T(8,128)} fusion(f32[2048,1024]{1,0:T(8,128)} %param.8, f32[128,1024]{1,0:T(8,128)S(1)} %fusion.53, f32[128,1024]{1,0:T(8,128)} %copy-done.3, f32[2048]{0:T(1024)S(1)} %bitcast.141, f32[]{:T(128)S(6)} %sqrt.3), kind=kOutput, calls=%fused_computation.10 | convolution fusion | flops 6443499520 | bytes 11542532 | tf_op jit(solution)/shard_map/dot_general | solution.py:12
  436.7 9.9 %fusion.4 = f32[2048,256]{0,1:T(8,128)S(1)} fusion(f32[2048,1024]{1,0:T(8,128)} %param.7, f32[128,1024]{1,0:T(8,128)S(1)} %fusion.54, f32[128,1024]{1,0:T(8,128)S(1)} %fusion.21, f32[2048]{0:T(1024)S(1)} %bitcast.142), kind=kOutput, calls=%fused_computation.12 | convolution fusion | flops 6443237376 | bytes 11542528 | tf_op jit(solution)/shard_map/dot_general | solution.py:12
  (91 shorter events, 42.9 us)
Async XLA Ops:
  7.2 179.5 %copy-start = (f32[1024,256]{1,0:T(8,128)S(1)}, f32[1024,256]{1,0:T(8,128)}, u32[]{:S(2)}) copy-start(f32[1024,256]{1,0:T(8,128)} %param.10) | copy-start | bytes 3145732
  7.2 179.5 %all-reduce.3.cloned.1.call-start = ((), (), s32[]{:S(2)}) async-start(), calls=%async_computation | async-start | bytes 8388608 | tf_op jit(solution)/shard_map/psum | solution.py:52
  186.7 9.1 %copy-start.1 = (f32[1024,1024]{0,1:T(8,128)S(1)}, f32[1024,1024]{0,1:T(8,128)}, u32[]{:S(2)}) copy-start(f32[1024,1024]{0,1:T(8,128)} %all-reduce.3.cloned.1.call-done) | copy-start | bytes 12582916
  261.5 10.4 %copy-start.2 = (f32[1024,1024]{0,1:T(8,128)S(1)}, f32[1024,1024]{0,1:T(8,128)}, u32[]{:S(2)}) copy-start(f32[1024,1024]{0,1:T(8,128)} %all-reduce.3.cloned.1.call-done) | copy-start | bytes 12582916
  353.1 0.7 copy-start.5
  389.3 2.7 copy-start.4
  396.9 0.7 copy-start.6
  418.6 0.8 copy-start.3
Sparse Core Ops, SparseCore 0:
  41.7 144.9 all-reduce.2
where the time goes:
time: 464 us; the launch traced here: 456 us
  other arithmetic  167 us (36%)
  waiting for transfers between devices  145 us (31%)
  matrix products  105 us (23%)
  between operations  20.1 us (4%)
  local copies, waits for them, and re-layouts  19.1 us (4%)
    psum x1, waiting for transfers between devices, local(): gram_matrix = lax.psum(gram_term(left_factor, masked_right), 'rows')  145 us
    another operation x13, other arithmetic, orthonormal(): factor = jnp.linalg.cholesky(transposed_product(block, block))  69.1 us
    another operation x7, other arithmetic, right_solve(): return jax.scipy.linalg.solve_triangular(factor, block.T, lower=True).T  60.9 us
    dot_general x5, matrix products, product(): jnp.dot(left_side, right_side, precision=lax.Precision.HIGHEST, preferred...  47.1 us
    dot_general x6, matrix products, transposed_product(): lax.dot_general(left_side, right_side, (((0,), (0,)), ((), ())), precisio...  45.8 us
    another operation x7, other arithmetic, local(): factor = jnp.linalg.cholesky(square)  34.8 us
    another operation x22, local copies, waits for them, and re-layouts, right_solve(): return jax.scipy.linalg.solve_triangular(factor, block.T, lower=True).T  11.6 us
  transfers between devices with their start and end apart: 1, of which 1 were waited for; matrix products, arithmetic and copies ran while one was open for 0% of the time, Pallas kernels for 0%

commit v1 on v0

v1 whole, which is shorter than its diff:
```python
import functools

import jax
import jax.numpy as jnp
from jax import lax
from jax.experimental import pallas as pl
from jax.experimental.pallas import tpu as pltpu
from jax.sharding import PartitionSpec as P

SLOTS = 4
POWER = 2
GROUP = 8
MESH = pl.DeviceIdType.MESH
NN = (((1,), (0,)), ((), ()))
NT = (((1,), (1,)), ((), ()))


def split(value):
    high = value.astype(jnp.bfloat16)
    return high, (value - high.astype(jnp.float32)).astype(jnp.bfloat16)


def dot_pairs(left, right, dims):
    one = lambda a, b: lax.dot_general(a, b, dims, preferred_element_type=jnp.float32)
    return one(left[0], right[0]) + (one(left[0], right[1]) + one(left[1], right[0]))


def full_dot(left, right, dims=NN):
    return lax.dot_general(
        left, right, dims, precision=lax.Precision.HIGHEST, preferred_element_type=jnp.float32
    )


def sum_kernel(chips, part, high, low, arrived, summed, gathered, total, d2d, rs, ag, fwd):
    me = lax.axis_index("rows")
    core = lax.rem(me, 2)
    chip = me // 2
    partner = me + 1 - 2 * core
    half = part.shape[0] // 2
    rows = half // chips

    def block(which, owner):
        return pl.ds(pl.multiple_of(which * half + owner * rows, GROUP), rows)

    def ahead(u):
        return lax.rem(chip + u, chips)

    def behind(u):
        return lax.rem(chip + chips - u, chips)

    def copy(src, dst, sems, u, device):
        return pltpu.make_async_remote_copy(
            src_ref=src,
            dst_ref=dst,
            send_sem=sems.at[0, u - 1],
            recv_sem=sems.at[1, u - 1],
            device_id=(device,),
            device_id_type=MESH,
        )

    def to_partner(u):
        return copy(part.at[block(1 - core, ahead(u))], arrived.at[u - 1], d2d, u, partner)

    def to_owner(u):
        return copy(summed.at[u - 1], gathered.at[u - 1], rs, u, 2 * ahead(u) + core)

    def to_peer(u):
        mine = block(core, chip)
        return copy(total.at[mine], total.at[mine], ag, u, 2 * ahead(u) + core)

    def from_peer(u):
        theirs = block(core, behind(u))
        return copy(total.at[theirs], total.at[theirs], ag, u, 2 * behind(u) + core)

    def pass_on(u):
        theirs = block(core, behind(u))
        return copy(total.at[theirs], total.at[theirs], fwd, u, partner)

    def from_partner(u):
        theirs = block(1 - core, behind(u))
        return copy(total.at[theirs], total.at[theirs], fwd, u, partner)

    def each(first, last, body):
        def step(u, carry):
            body(u)
            return carry

        lax.fori_loop(first, last, step, 0)

    def put(where):
        pair = split(total[where])
        high[where] = pair[0]
        low[where] = pair[1]

    barrier = pltpu.get_barrier_semaphore()
    pl.semaphore_signal(barrier, inc=1, device_id=(partner,), device_id_type=MESH)
    each(
        1,
        chips,
        lambda u: pl.semaphore_signal(
            barrier, inc=1, device_id=(2 * ahead(u) + core,), device_id_type=MESH
        ),
    )
    pl.semaphore_wait(barrier, chips)

    each(1, chips + 1, lambda u: to_partner(u).start())

    def reduce_pair(u):
        to_partner(u).wait_recv()
        summed[u - 1] = part[block(core, ahead(u))] + arrived[u - 1]
        to_owner(u).start()

    each(1, chips, reduce_pair)
    to_partner(chips).wait_recv()
    mine = block(core, chip)
    total[mine] = part[mine] + arrived[chips - 1]

    def accumulate(u):
        to_owner(u).wait_recv()
        total[mine] += gathered[u - 1]

    each(1, chips, accumulate)
    each(1, chips, lambda u: to_peer(u).start())
    pass_on(chips).start()
    put(mine)

    def relay(u):
        from_peer(u).wait_recv()
        pass_on(u).start()
        put(block(core, behind(u)))

    each(1, chips, relay)
    from_partner(chips).wait_recv()
    put(block(1 - core, chip))

    def take(u):
        from_partner(u).wait_recv()
        put(block(1 - core, behind(u)))

    each(1, chips, take)
    each(1, chips + 1, lambda u: to_partner(u).wait_send())
    each(1, chips, lambda u: to_owner(u).wait_send())
    each(1, chips, lambda u: to_peer(u).wait_send())
    each(1, chips + 1, lambda u: pass_on(u).wait_send())


def sum_over_devices(part, devices):
    chips = devices // 2
    size, width = part.shape
    rows = size // devices
    block = pltpu.VMEM((chips, rows, width), jnp.float32)
    vmem = pl.BlockSpec(memory_space=pltpu.VMEM)
    sems = pltpu.SemaphoreType.DMA((2, chips))
    return pl.pallas_call(
        functools.partial(sum_kernel, chips),
        out_shape=[jax.ShapeDtypeStruct(part.shape, jnp.bfloat16)] * 2,
        in_specs=[vmem],
        out_specs=[vmem, vmem],
        scratch_shapes=[block, block, block, pltpu.VMEM(part.shape, jnp.float32), sems, sems, sems, sems],
        compiler_params=pltpu.CompilerParams(
            collective_id=0, has_side_effects=True, vmem_limit_bytes=40 * 2**20
        ),
        name="sum_over_devices",
    )(part)


def inverse_factor(matrix):
    size = matrix.shape[0]
    groups = size // GROUP
    shape = (GROUP, size)
    row_ids = lax.broadcasted_iota(jnp.int32, shape, 0)
    lane_ids = lax.broadcasted_iota(jnp.int32, shape, 1)
    wide = lambda v: jnp.broadcast_to(v, shape)
    left = [matrix[GROUP * g : GROUP * (g + 1), :] for g in range(groups)]
    right = [jnp.where(lane_ids == row_ids + GROUP * g, 1.0, 0.0) for g in range(groups)]
    for g in range(groups):
        panel, beside = left[g], right[g]
        entry, factor, inverse, scale = {}, {}, {}, {}
        for j in range(GROUP):
            column = wide(panel[:, GROUP * g + j : GROUP * g + j + 1])
            for i in range(j, GROUP):
                entry[i, j] = wide(column[i : i + 1, :])
        for j in range(GROUP):
            scale[j] = lax.rsqrt(entry[j, j])
            for i in range(j + 1, GROUP):
                factor[i, j] = entry[i, j] * scale[j]
            for l in range(j + 1, GROUP):
                for i in range(l, GROUP):
                    entry[i, l] = entry[i, l] - factor[i, j] * factor[l, j]
        for j in range(GROUP):
            inverse[j, j] = scale[j]
            for i in range(j + 1, GROUP):
                acc = factor[i, j] * inverse[j, j]
                for l in range(j + 1, i):
                    acc = acc + factor[i, l] * inverse[l, j]
                inverse[i, j] = -acc * scale[i]
        new_panel, new_beside = jnp.zeros(shape, jnp.float32), jnp.zeros(shape, jnp.float32)
        for j in range(GROUP):
            column = jnp.zeros(shape, jnp.float32)
            for i in range(j, GROUP):
                column = jnp.where(row_ids == i, inverse[i, j], column)
            new_panel = new_panel + column * wide(panel[j : j + 1, :])
            new_beside = new_beside + column * wide(beside[j : j + 1, :])
        right[g] = new_beside
        if g + 1 < groups:
            turned = new_panel.T
            rows_of = [wide(new_panel[j : j + 1, :]) for j in range(GROUP)]
            beside_of = [wide(new_beside[j : j + 1, :]) for j in range(GROUP)]
            for r in range(g + 1, groups):
                tile = turned[GROUP * r : GROUP * (r + 1), :]
                for j in range(GROUP):
                    weight = wide(tile[:, j : j + 1])
                    left[r] = left[r] - weight * rows_of[j]
                    right[r] = right[r] - weight * beside_of[j]
    return jnp.concatenate(right, axis=0)


def chain_kernel(start, high, low, left_map, right_map, basis, image, square, inverse):
    rank = start.shape[0]
    cut = rank // 2
    basis[...] = start[...]
    inverse[...] = jnp.zeros_like(inverse)

    def turn(iteration, carry):
        gram = (high[...], low[...])
        image[...] = dot_pairs(split(basis[...]), gram, NT)

        @pl.when(iteration < POWER)
        def _():
            image[...] = dot_pairs(split(image[...]), (high[...], low[...]), NN)

        pair = split(image[...])
        square[...] = dot_pairs(pair, pair, NT)
        first = inverse_factor(square[:cut, :cut])
        across = full_dot(first, square[:cut, cut:])
        across_t = across.T
        second = inverse_factor(square[cut:, cut:] - full_dot(across_t, across))
        inverse[:cut, :cut] = first
        inverse[cut:, cut:] = second
        inverse[cut:, :cut] = -full_dot(second, full_dot(across_t, first))
        solved = split(inverse[...])

        @pl.when(iteration == POWER)
        def _():
            shape = square.shape
            diagonal = lax.broadcasted_iota(jnp.int32, shape, 0) == lax.broadcasted_iota(jnp.int32, shape, 1)
            trace = jnp.sum(jnp.where(diagonal, square[...], 0.0), keepdims=True)
            scaling = jnp.sqrt(trace / rank)
            right_map[...] = dot_pairs(solved, split(basis[...]), NN) * scaling
            left_map[...] = dot_pairs(solved, pair, NN)

        @pl.when(iteration < POWER)
        def _():
            basis[...] = dot_pairs(solved, pair, NN)

        return carry

    lax.fori_loop(0, POWER + 1, turn, 0)


def maps_of(start_rows, high, low):
    rank, states = start_rows.shape
    vmem = pl.BlockSpec(memory_space=pltpu.VMEM)
    small = pltpu.VMEM((rank, rank), jnp.float32)
    wide = pltpu.VMEM((rank, states), jnp.float32)
    return pl.pallas_call(
        chain_kernel,
        out_shape=[jax.ShapeDtypeStruct((rank, states), jnp.float32)] * 2,
        in_specs=[vmem] * 3,
        out_specs=[vmem] * 2,
        scratch_shapes=[wide, wide, small, small],
        compiler_params=pltpu.CompilerParams(vmem_limit_bytes=40 * 2**20),
        name="maps_of",
    )(start_rows, high, low)


def project(factor_rows, mapping, row_mask):
    rows = lax.dot_general(
        factor_rows, mapping, NT, precision=lax.Precision.HIGH, preferred_element_type=jnp.float32
    )
    return rows * row_mask


def local(devices, left_factor, right_factor, tile_counts, start_basis):
    tile_rows = left_factor.shape[0] // SLOTS
    live_count = tile_counts[0]
    slot_ids = lax.broadcasted_iota(jnp.int32, (SLOTS, 1, 1), 0)
    live_slots = (slot_ids < live_count).astype(jnp.float32)
    row_mask = jnp.broadcast_to(live_slots, (SLOTS, tile_rows, 1)).reshape(-1, 1)
    part = lax.dot_general(
        left_factor,
        right_factor * row_mask,
        (((0,), (0,)), ((), ())),
        precision=lax.Precision.HIGH,
        preferred_element_type=jnp.float32,
    )
    high, low = sum_over_devices(part, devices)
    left_map, right_map = maps_of(start_basis.T, high, low)
    return project(left_factor, left_map, row_mask), project(right_factor, right_map, row_mask)


def solution(mesh):
    return jax.shard_map(
        functools.partial(local, mesh.shape["rows"]),
        mesh=mesh,
        in_specs=(P("rows", None), P("rows", None), P("rows"), P()),
        out_specs=(P("rows", None), P("rows", None)),
        check_vma=False,
    )
```

time: 464 us -> 210 us (0.45)
  the two profiles are of different devices: /device:TPU:0 before, /device:TPU:31 now
where the time goes in v1:
time: 210 us; the launch traced here: 209 us
  Pallas kernels  168 us (80%)
  matrix products  30.7 us (15%)
  local copies, waits for them, and re-layouts  9.13 us (4%)
    pallas_call x1, Pallas kernels, sum_over_devices(): pl.pallas_call(functools.partial(sum_kernel, chips), out_shape=[jax.Shape...  115 us
    pallas_call x1, Pallas kernels, maps_of(): pl.pallas_call(chain_kernel, out_shape=[jax.ShapeDtypeStruct((rank, state...  53.2 us
    dot_general x1, matrix products, local(): lax.dot_general(left_factor, right_factor * row_mask, (((0,), (0,)), ((),...  18.6 us
    dot_general x2, matrix products, project(): lax.dot_general(factor_rows, mapping, NT, precision=lax.Precision.HIGH, p...  12.2 us
    unnamed x13, local copies, waits for them, and re-layouts  9.13 us

profile of v1, /device:TPU:31, one launch (start us, length us, event | category | flops | bytes accessed | tf_op | source)
XLA Modules:
  0.0 209.4 jit_solution(1103586273838864151)
XLA Ops:
  1.3 0.1 broadcast_bitcast_fusion
  1.4 18.6 %fusion.5.part = f32[1024,1024]{1,0:T(8,128)S(1)} fusion(f32[2048,1024]{1,0:T(8,128)} %param.4, f32[2048,1024]{1,0:T(8,128)} %param.5, f32[2048]{0:T(1024)S(1)} %bitcast.18), kind=kOutput, calls=%fused_computation.7 | convolution fusion | flops 12886999040 | bytes 20979712 | tf_op jit(solution)/shard_map/dot_general | solution.py:290
  19.9 115.1 %sum_over_devices.1 = (bf16[1024,1024]{1,0:T(8,128)(2,1)S(1)}, bf16[1024,1024]{1,0:T(8,128)(2,1)S(1)}) custom-call(f32[1024,1024]{1,0:T(8,128)S(1)} %fusion.5.part), custom_call_target="tpu_custom_call" | custom-call | tf_op jit(solution)/shard_map/sum_over_devices/pallas_call | solution.py:154
  135.0 0.0 copy-start
  135.0 1.3 copy-done
  136.3 1.6 copy.6
  137.9 0.0 copy-start.1
  137.9 1.6 copy-done.1
  139.5 53.2 %maps_of.1 = (f32[256,1024]{1,0:T(8,128)S(1)}, f32[256,1024]{1,0:T(8,128)S(1)}) custom-call(f32[256,1024]{1,0:T(8,128)S(1)} %bitcast.17, bf16[1024,1024]{1,0:T(8,128)(2,1)S(1)} %get-tuple-element.6.high, bf16[1024,1024]{1,0:T(8,128)(2,1)S(1)} %copy-done.1), custom_call_target="tpu_custom_call" | custom-call | tf_op jit(solution)/shard_map/maps_of/pallas_call | solution.py:266
  192.6 0.0 copy-start.2
  192.6 1.0 copy-done.2
  193.6 0.0 copy-start.3
  193.6 6.1 %fusion.3 = f32[2048,256]{0,1:T(8,128)S(1)} fusion(f32[256,1024]{1,0:T(8,128)S(1)} %get-tuple-element.9, f32[2048,1024]{1,0:T(8,128)} %param.5, f32[2048]{0:T(1024)S(1)} %bitcast.19), kind=kOutput, calls=%fused_computation.4 | convolution fusion | flops 3221749760 | bytes 11542528 | tf_op jit(solution)/shard_map/dot_general | solution.py:278
  199.8 1.8 copy.9
  201.6 0.0 copy-done.3
  201.6 6.0 %fusion.4 = f32[2048,256]{0,1:T(8,128)S(1)} fusion(f32[256,1024]{1,0:T(8,128)S(1)} %copy-done.3, f32[2048,1024]{1,0:T(8,128)} %param.4, f32[2048]{0:T(1024)S(1)} %bitcast.20), kind=kOutput, calls=%fused_computation.6 | convolution fusion | flops 3221749760 | bytes 11542528 | tf_op jit(solution)/shard_map/dot_general | solution.py:278
  207.6 1.8 copy.8
  (2 shorter events, 0.0 us)
Async XLA Ops:
  135.0 1.3 copy-start
  137.9 1.6 copy-start.1
  192.6 1.0 copy-start.2
  193.6 8.0 %copy-start.3 = (f32[256,1024]{1,0:T(8,128)S(1)}, f32[256,1024]{1,0:T(8,128)}, u32[]{:S(2)}) copy-start(f32[256,1024]{1,0:T(8,128)} %copy-done.2) | copy-start | bytes 3145732
